TPU v7x, 32 devices: a whole 2x2x4 slice. The times are simulated.
32 devices in a mesh: blk: 8 (over y, x, core), ulysses: 4 (over z).
Axes of the slice: x: 2, y: 2, z: 4, core: 2. Of those that a mesh axis runs over, the one named last changes fastest.
Arguments:
- tokens: bfloat16 [2048, 3072], P(('blk', 'ulysses')), may hold values from -6 to 6
- mod_shift: float32 [3072], replicated, may hold values from -3 to 3
- mod_scale: float32 [3072], replicated, may hold values from -3 to 3
- mod_gate: float32 [3072], replicated, may hold values from 0.5 to 1.5
- qkv_weight: bfloat16 [3, 3072, 3072], P(None, None, 'ulysses'), may hold values from -0.109375 to 0.109375
- query_gain: float32 [128], replicated, may hold values from 1 to 16
- key_gain: float32 [128], replicated, may hold values from 1 to 16
- out_weight: bfloat16 [3072, 3072], P(None, 'ulysses'), may hold values from -0.109375 to 0.109375
Outputs:
- mixed: bfloat16 [2048, 3072], P(('blk', 'ulysses'))
All inputs are finite; a program needn't handle non-finite values.
Results may differ from a plain program's by a relative error of at most 0.013.
The roundings to bfloat16 on the way count: a program that leaves them out, or rounds other values in their place, can miss the bound.
Values may be sent and summed in bfloat16 or wider, within the bound.
No kernel may reach another device: no remote copies, remote signals or barrier semaphores. Data moves between devices by JAX's collectives and lax.ppermute only.
A program may use at most 128 MiB of HBM per device.

v0:
```python
import math
import jax
import jax.numpy as jnp
from jax import lax
from jax.sharding import PartitionSpec as P


def head_norm(projected, gain, factor):
    split = projected.reshape(projected.shape[0], -1, gain.shape[0])
    meansq = jnp.mean(split * split, axis=-1, keepdims=True)
    return (split * lax.rsqrt(meansq + 1e-06) * gain * factor).reshape(projected.shape)


def local(tokens, mod_shift, mod_scale, mod_gate, qkv_weight, query_gain, key_gain, out_weight):
    wide = tokens.astype(jnp.float32)
    center = jnp.mean(wide, axis=-1, keepdims=True)
    spread = jnp.mean((wide - center) ** 2, axis=-1, keepdims=True)
    normed = (wide - center) / jnp.sqrt(spread + 1e-06)
    modulated = (normed * (1.0 + mod_scale) + mod_shift).astype(jnp.bfloat16)
    head_size = query_gain.shape[0]
    local_width = qkv_weight.shape[2]
    heads_here = local_width // head_size
    factor = 1.0 / math.sqrt(head_size)
    sums = jnp.einsum(
        "rd,jde->jre",
        lax.all_gather(modulated, "ulysses", axis=0, tiled=True),
        qkv_weight,
        preferred_element_type=jnp.float32,
    )
    queries = head_norm(sums[0], query_gain, factor)
    keys = head_norm(sums[1], key_gain, 1.0)
    stacked = jnp.stack([queries, keys, sums[2]]).astype(jnp.bfloat16)
    queries, keys, values = (stacked[0], stacked[1], stacked[2])
    query_rows = queries.shape[0]
    query_heads = queries.reshape(query_rows, heads_here, head_size)
    start_state = (
        jnp.full((heads_here, query_rows), -1e30, jnp.float32),
        jnp.zeros((heads_here, query_rows), jnp.float32),
        jnp.zeros((heads_here, query_rows, head_size), jnp.float32),
    )
    key_part = lax.all_gather(keys, "blk", axis=0, tiled=True)
    value_part = lax.all_gather(values, "blk", axis=0, tiled=True)
    count = key_part.shape[0] // query_rows

    def step(position, state):
        highest, total, numerator = state
        key_block = lax.dynamic_slice_in_dim(key_part, position * query_rows, query_rows, 0)
        value_block = lax.dynamic_slice_in_dim(value_part, position * query_rows, query_rows, 0)
        key_block = key_block.reshape(query_rows, heads_here, head_size)
        value_block = value_block.reshape(query_rows, heads_here, head_size)
        scores = jnp.einsum(
            "qhd,khd->hqk", query_heads, key_block, preferred_element_type=jnp.float32
        )
        new_high = jnp.maximum(highest, jnp.max(scores, axis=-1))
        rescale = jnp.exp(highest - new_high)
        powers = jnp.exp(scores - new_high[..., None])
        total = total * rescale + jnp.sum(powers, axis=-1)
        numerator = numerator * rescale[..., None] + jnp.einsum(
            "hqk,khd->hqd",
            powers.astype(jnp.bfloat16),
            value_block,
            preferred_element_type=jnp.float32,
        )
        return (new_high, total, numerator)

    highest, total, numerator = lax.fori_loop(0, count, step, start_state)
    attended = (numerator / total[..., None]).transpose(1, 0, 2).reshape(query_rows, local_width)
    attended = attended.astype(jnp.bfloat16)
    columns = jnp.dot(
        lax.all_gather(attended, "ulysses", axis=1, tiled=True),
        out_weight,
        preferred_element_type=jnp.float32,
    )
    branch = lax.all_to_all(
        columns.astype(jnp.bfloat16), "ulysses", split_axis=0, concat_axis=1, tiled=True
    ).astype(columns.dtype)
    return (wide + mod_gate * branch).astype(jnp.bfloat16)


def solution(mesh):
    in_specs = (
        P(("blk", "ulysses"), None),
        P(),
        P(),
        P(),
        P(None, None, "ulysses"),
        P(),
        P(),
        P(None, "ulysses"),
    )
    out_specs = P(("blk", "ulysses"), None)
    return jax.shard_map(local, mesh=mesh, in_specs=in_specs, out_specs=out_specs, check_vma=False)
```

profile of v0, /device:TPU:0, one launch (start us, length us, event | category | flops | bytes accessed | tf_op | source)
XLA Modules:
  0.0 214.0 jit_solution(12685129563109106059)
XLA Ops:
  6.5 1.1 convert_reduce_fusion
  7.7 1.3 fusion.9
  9.0 0.7 broadcast_add_fusion
  9.7 2.0 fusion.12
  11.8 39.8 %all-gather.7.cloned.1.call-done = bf16[256,3072]{1,0:T(8,128)(2,1)} async-done(((bf16[64,3072]{1,0:T(8,128)(2,1)}), bf16[256,3072]{1,0:T(8,128)(2,1)}) %all-gather.7.cloned.1.call-update) | async-done | bytes 1572880 | tf_op jit(solution)/shard_map/all_gather | solution.py:26
  51.6 7.9 %convolution_bitcast_fusion = f32[3,256,768]{2,1,0:T(8,128)S(1)} fusion(bf16[3,3072,768]{2,1,0:T(8,128)(2,1)} %param.14, bf16[256,3072]{1,0:T(8,128)(2,1)} %all-gather.7.cloned.1.call-done), kind=kOutput, calls=%fused_computation.14 | convolution fusion | flops 3623878656 | bytes 18087936 | tf_op jit(solution)/shard_map/rd,jde->jre/dot_general | solution.py:24
  59.5 0.8 slice.32
  60.3 1.2 slice_multiply_fusion
  61.6 1.4 copy.30
  63.1 1.2 copy.31
  64.3 1.4 copy.28
  65.9 1.1 copy.29
  67.0 2.4 %multiply_convert_fusion = (bf16[1,256,768]{2,1,0:T(8,128)(2,1)S(1)}, bf16[1,256,768]{2,1,0:T(8,128)(2,1)}) fusion(f32[1,256,768]{2,1,0:T(8,128)} %copy.31, f32[3,256,768]{2,1,0:T(8,128)S(1)} %convolution_bitcast_fusion, f32[768]{0:T(1024)S(1)} %get-tuple-element.201, f32[768]{0:T(1024)S(1)} %get-tuple-element.202, f32[1,256,768]{2,1,0:T(8,128)} %copy.29), kind=kLoop, calls=%fused_computation.30 | loop fusion | flops 1376256 | bytes 3938304 | tf_op jit(solution)/shard_map/slice | solution.py:33
  69.9 21.6 %all-gather.13.cloned.1.call-done = bf16[1,2048,768]{2,1,0:T(8,128)(2,1)} async-done(((bf16[1,256,768]{2,1,0:T(8,128)(2,1)}), bf16[1,2048,768]{2,1,0:T(8,128)(2,1)}) %all-gather.13.cloned.1.call-update) | async-done | bytes 3145744 | tf_op jit(solution)/shard_map/all_gather | solution.py:42
  91.5 34.1 %all-gather.11.cloned.1.call-done = bf16[1,2048,768]{2,1,0:T(8,128)(2,1)} async-done(((bf16[1,256,768]{2,1,0:T(8,128)(2,1)}), bf16[1,2048,768]{2,1,0:T(8,128)(2,1)}) %all-gather.11.cloned.1.call-update) | async-done | bytes 3145744 | tf_op jit(solution)/shard_map/all_gather | solution.py:41
  125.6 23.6 %while.18 = (s32[]{:T(128)}, f32[6,256]{1,0:T(8,128)S(1)}, f32[6,256]{1,0:T(8,128)S(1)}, f32[6,256,128]{2,1,0:T(8,128)S(1)}, bf16[2048,768]{1,0:T(8,128)(2,1)}, ...) while((s32[]{:T(128)}, f32[6,256]{1,0:T(8,128)S(1)}, ...), condition=%wide.region_7.0_spmd.clone, body=%wide.region_4.0_spmd.clone.sunk | while | flops 203890176 | bytes 10715315 | solution.py:66
  125.6 1.2 constant_dynamic-slice_fusion.3
  127.1 0.4 bitcast_reduce_fusion.2
  127.8 0.7 convolution_add_fusion.2
  128.5 1.2 constant_dynamic-slice_fusion.3
  130.0 0.4 bitcast_reduce_fusion.2
  130.5 0.2 fusion.30
  130.7 0.7 convolution_add_fusion.2
  131.5 1.2 constant_dynamic-slice_fusion.3
  133.0 0.4 bitcast_reduce_fusion.2
  133.7 0.7 convolution_add_fusion.2
  134.4 1.2 constant_dynamic-slice_fusion.3
  135.9 0.4 bitcast_reduce_fusion.2
  136.6 0.7 convolution_add_fusion.2
  137.4 1.2 constant_dynamic-slice_fusion.3
  138.9 0.4 bitcast_reduce_fusion.2
  139.6 0.7 convolution_add_fusion.2
  140.3 1.2 constant_dynamic-slice_fusion.3
  141.8 0.4 bitcast_reduce_fusion.2
  142.5 0.7 convolution_add_fusion.2
  143.3 1.2 constant_dynamic-slice_fusion.3
  144.8 0.4 bitcast_reduce_fusion.2
  145.5 0.7 convolution_add_fusion.2
  146.2 1.2 constant_dynamic-slice_fusion.3
  147.7 0.4 bitcast_reduce_fusion.2
  148.4 0.7 convolution_add_fusion.2
  149.1 0.3 copy.36
  149.4 0.8 divide_convert_fusion
  150.2 37.2 %all-gather.9.cloned.1.call-done = bf16[256,3072]{0,1:T(8,128)(2,1)} async-done(((bf16[256,768]{0,1:T(8,128)(2,1)}), bf16[256,3072]{0,1:T(8,128)(2,1)}) %all-gather.9.cloned.1.call-update) | async-done | bytes 1572880 | tf_op jit(solution)/shard_map/all_gather | solution.py:70
  187.4 4.2 %convolution_convert_fusion = bf16[256,768]{1,0:T(8,128)(2,1)S(1)} fusion(bf16[256,3072]{0,1:T(8,128)(2,1)} %all-gather.9.cloned.1.call-done, bf16[3072,768]{1,0:T(8,128)(2,1)} %param.17), kind=kOutput, calls=%fused_computation.16 | convolution fusion | flops 1208156160 | bytes 6684672 | tf_op jit(solution)/shard_map/dot_general | solution.py:69
  191.7 13.9 %all_to_all.13 = bf16[4,64,768]{2,1,0:T(8,128)(2,1)S(1)} all-to-all(bf16[4,64,768]{2,1,0:T(8,128)(2,1)S(1)} %bitcast.69), channel_id=1, replica_groups=mesh['blk'=8,'ulysses'=4] {'ulysses'}, dimensions={0} | all-to-all | bytes 786432 | tf_op jit(solution)/shard_map/all_to_all | solution.py:74
  205.7 0.9 copy-done
  206.6 0.8 fusion.13
  (78 shorter events, 5.4 us)
Async XLA Ops:
  6.5 45.1 %all-gather.7.cloned.1.call-start = ((), (), s32[]{:S(2)}) async-start(), calls=%async_computation.1 | async-start | bytes 1966080 | tf_op jit(solution)/shard_map/all_gather | solution.py:26
  11.7 48.6 %copy-start.2 = (f32[128]{0:T(128)S(1)}, f32[128]{0:T(128)}, u32[]{:S(2)}) copy-start(f32[128]{0:T(128)} %param.15) | copy-start | bytes 1540
  11.7 48.6 %copy-start.3 = (f32[128]{0:T(128)S(1)}, f32[128]{0:T(128)}, u32[]{:S(2)}) copy-start(f32[128]{0:T(128)} %param.16) | copy-start | bytes 1540
  11.7 79.8 %all-gather.13.cloned.1.call-start = ((), (), s32[]{:S(2)}) async-start(), calls=%async_computation.4 | async-start | bytes 3538944 | tf_op jit(solution)/shard_map/all_gather | solution.py:42
  60.3 65.3 %all-gather.11.cloned.1.call-start = ((), (), s32[]{:S(2)}) async-start(), calls=%async_computation.3 | async-start | bytes 3538944 | tf_op jit(solution)/shard_map/all_gather | solution.py:41
  69.4 118.0 %all-gather.9.cloned.1.call-start = ((), (), s32[]{:S(2)}) async-start(), calls=%async_computation.2 | async-start | bytes 1966080 | tf_op jit(solution)/shard_map/all_gather | solution.py:70
  205.6 1.0 copy-start
  205.6 1.0 copy-start.1
Sparse Core Ops, SparseCore 0:
  11.8 39.7 all-gather.6
  60.4 31.0 all-gather.12
  93.4 32.1 all-gather.10
  150.4 37.0 all-gather.8
where the time goes:
time: 215 us; the launch traced here: 214 us
  waiting for transfers between devices  133 us (62%)
  matrix products  21 us (10%)
  local copies, waits for them, and re-layouts  19.7 us (9%)
  blocking collectives  13.9 us (6%)
  between operations  13.3 us (6%)
  other arithmetic  12.5 us (6%)
    all_gather x1, waiting for transfers between devices, local(): lax.all_gather(modulated, 'ulysses', axis=0, tiled=True)  39.8 us
    all_gather x1, waiting for transfers between devices, local(): lax.all_gather(attended, 'ulysses', axis=1, tiled=True)  37.2 us
    all_gather x1, waiting for transfers between devices, local(): key_part = lax.all_gather(keys, 'blk', axis=0, tiled=True)  34.1 us
    all_gather x1, waiting for transfers between devices, local(): value_part = lax.all_gather(values, 'blk', axis=0, tiled=True)  21.6 us
    all_to_all x1, blocking collectives, local(): lax.all_to_all(columns.astype(jnp.bfloat16), 'ulysses', split_axis=0, con...  13.9 us
    dynamic_slice x16, local copies, waits for them, and re-layouts, step(): lax.dynamic_slice_in_dim(value_part, position * query_rows, query_rows, 0)  10.7 us
    dot_general x1, matrix products, local(): jnp.einsum('rd,jde->jre', lax.all_gather(modulated, 'ulysses', axis=0, ti...  7.86 us
    dot_general x8, matrix products, step(): jnp.einsum('hqk,khd->hqd', powers.astype(jnp.bfloat16), value_block, pref...  5.52 us
  transfers between devices with their start and end apart: 4, of which 4 were waited for; matrix products, arithmetic and copies ran while one was open for 4% of the time, Pallas kernels for 0%

commit v1 on v0

--- a/solution.py
+++ b/solution.py
@@ -3,6 +3,29 @@
 import jax.numpy as jnp
 from jax import lax
 from jax.sharding import PartitionSpec as P
+
+
+def trace_series_all(arr_in, dim_i):
+    arr_in = jnp.moveaxis(arr_in, 0, dim_i)
+    x_new = arr_in.shape
+    part_now = arr_in.reshape(*x_new[:dim_i], x_new[dim_i] * x_new[dim_i + 1], *x_new[dim_i + 2 :])
+    return part_now
+
+
+def serve_ticks_in(v0, axis_key, axis_k, original, on_dim=1):
+    block_out = lax.axis_index(axis_key)
+    z2 = lax.axis_size(axis_key)
+    oldest, x_next, later = (z2, block_out, v0.shape[axis_k])
+    leaves = [(k0, (k0 + 1) % oldest) for k0 in range(oldest)]
+    t_next = v0
+    queue = []
+    for w in range(oldest):
+        e_now = t_next if w == oldest - 1 else lax.ppermute(t_next, axis_key, leaves)
+        queue.append(original(t_next, (x_next - w) % oldest * later))
+        t_next = e_now
+    queue = jnp.stack(queue, axis=0)[(x_next - jnp.arange(oldest)) % oldest]
+    mixed_arr = trace_series_all(queue, on_dim)
+    return mixed_arr
 
 
 def head_norm(projected, gain, factor):
@@ -21,11 +44,13 @@
     local_width = qkv_weight.shape[2]
     heads_here = local_width // head_size
     factor = 1.0 / math.sqrt(head_size)
-    sums = jnp.einsum(
-        "rd,jde->jre",
-        lax.all_gather(modulated, "ulysses", axis=0, tiled=True),
-        qkv_weight,
-        preferred_element_type=jnp.float32,
+    sums = serve_ticks_in(
+        modulated,
+        "ulysses",
+        0,
+        lambda own_block, offset: jnp.einsum(
+            "rd,jde->jre", own_block, qkv_weight, preferred_element_type=jnp.float32
+        ),
     )
     queries = head_norm(sums[0], query_gain, factor)
     keys = head_norm(sums[1], key_gain, 1.0)

time: 215 us -> 206 us (0.958)
  waiting for transfers between devices: 133 us -> 107 us
  matrix products: 21 us -> 38.5 us
  local copies, waits for them, and re-layouts: 19.7 us -> 16.1 us
  starting transfers between devices: 0.13 us -> 3.38 us
    all_gather x1 -> x0, waiting for transfers between devices: 39.8 us -> none  [local(): lax.all_gather(modulated, 'ulysses', axis=0, tiled=True)]
    dot_general x1 -> x4, matrix products: 7.86 us -> 25.4 us  [local(): jnp.einsum('rd,jde->jre', own_block, qkv_weight, preferred_element_type=j...]
    ppermute x0 -> x3, waiting for transfers between devices: none -> 11.5 us  [serve_ticks_in(): lax.ppermute(t_next, axis_key, leaves)]
    ppermute x0 -> x3, starting transfers between devices: none -> 3.11 us  [serve_ticks_in(): lax.ppermute(t_next, axis_key, leaves)]
    mul x2, local copies, waits for them, and re-layouts: 2.79 us -> 0.24 us  [head_norm(): meansq = jnp.mean(split * split, axis=-1, keepdims=True)]
    mul x5 -> x2, local copies, waits for them, and re-layouts: 2.42 us -> 0.01 us  [head_norm(): split * lax.rsqrt(meansq + 1e-06) * gain * factor]
    gather x0 -> x1, local copies, waits for them, and re-layouts: none -> 2.18 us  [serve_ticks_in(): queue = jnp.stack(queue, axis=0)[(x_next - jnp.arange(oldest)) % oldest]]
    dynamic_slice x16 -> x8, local copies, waits for them, and re-layouts: 10.7 us -> 9.42 us  [step(): lax.dynamic_slice_in_dim(value_part, position * query_rows, query_rows, 0)]
  transfers between devices with their start and end apart: 4 -> 6, of which waited for: 4 -> 6; matrix products, arithmetic and copies ran while one was open for 4% -> 14% of each run, Pallas kernels for 0% -> 0%
where the time goes in v1:
time: 206 us
  waiting for transfers between devices  107 us (52%)
  matrix products  38.5 us (19%)
  local copies, waits for them, and re-layouts  16.1 us (8%)
  blocking collectives  14.1 us (7%)
  between operations  13.4 us (7%)
  other arithmetic  12.9 us (6%)
  starting transfers between devices  3.38 us (2%)
    all_gather x1, waiting for transfers between devices, local(): lax.all_gather(attended, 'ulysses', axis=1, tiled=True)  37.2 us
    all_gather x1, waiting for transfers between devices, local(): key_part = lax.all_gather(keys, 'blk', axis=0, tiled=True)  34.6 us
    dot_general x4, matrix products, local(): jnp.einsum('rd,jde->jre', own_block, qkv_weight, preferred_element_type=j...  25.4 us
    all_gather x1, waiting for transfers between devices, local(): value_part = lax.all_gather(values, 'blk', axis=0, tiled=True)  23.5 us
    all_to_all x1, blocking collectives, local(): lax.all_to_all(columns.astype(jnp.bfloat16), 'ulysses', split_axis=0, con...  14.1 us
    ppermute x3, waiting for transfers between devices, serve_ticks_in(): lax.ppermute(t_next, axis_key, leaves)  11.5 us
    dynamic_slice x8, local copies, waits for them, and re-layouts, step(): lax.dynamic_slice_in_dim(value_part, position * query_rows, query_rows, 0)  9.42 us
    dot_general x8, matrix products, step(): jnp.einsum('hqk,khd->hqd', powers.astype(jnp.bfloat16), value_block, pref...  5.48 us
  transfers between devices with their start and end apart: 6, of which 6 were waited for; matrix products, arithmetic and copies ran while one was open for 14% of the time, Pallas kernels for 0%

profile of v1, /device:TPU:0, one launch (start us, length us, event | category | flops | bytes accessed | tf_op | source)
XLA Modules:
  0.0 205.8 jit_solution(5974549184022640450)
XLA Ops:
  6.5 1.2 convert_reduce_fusion
  7.7 1.3 fusion.8
  9.0 0.7 broadcast_add_fusion
  9.7 1.2 fusion.11
  10.9 3.1 %collective-permute-start = (bf16[64,3072]{1,0:T(8,128)(2,1)S(1)}, bf16[64,3072]{1,0:T(8,128)(2,1)S(1)}, u32[]{:S(2)}, u32[]{:S(2)}) collective-permute-start(bf16[64,3072]{1,0:T(8,128)(2,1)S(1)} %fusion.11), channel_id=1, source_target_pairs={{0,1},{1,2},{2,3},{3,0},{4,5},{5,6},{6,7},{7,4},{8,9},{9,10},{10,1... | collective-permute-start | bytes 1179656 | tf_op jit(solution)/shard_map/ppermute | solution.py:23
  14.0 7.6 %convolution_bitcast_fusion.3 = f32[1,3,64,768]{3,2,1,0:T(8,128)S(1)} fusion(bf16[3,3072,768]{2,1,0:T(8,128)(2,1)} %param.14, bf16[64,3072]{1,0:T(8,128)(2,1)S(1)} %fusion.11), kind=kOutput, calls=%fused_computation.20 | convolution fusion | flops 905969664 | bytes 15138816 | tf_op jit(solution)/shard_map/rd,jde->jre/dot_general | solution.py:51
  21.6 3.5 %collective-permute-done = bf16[64,3072]{1,0:T(8,128)(2,1)S(1)} collective-permute-done((bf16[64,3072]{1,0:T(8,128)(2,1)S(1)}, bf16[64,3072]{1,0:T(8,128)(2,1)S(1)}, u32[]{:S(2)}, u32[]{:S(2)}) %collective-permute-start) | collective-permute-done | bytes 393248 | tf_op jit(solution)/shard_map/ppermute | solution.py:23
  25.2 7.7 %convolution_bitcast_fusion.2 = f32[1,3,64,768]{3,2,1,0:T(8,128)S(1)} fusion(bf16[3,3072,768]{2,1,0:T(8,128)(2,1)} %param.14, bf16[64,3072]{1,0:T(8,128)(2,1)S(1)} %collective-permute-done), kind=kOutput, calls=%fused_computation.19 | convolution fusion | flops 905969664 | bytes 15138816 | tf_op jit(solution)/shard_map/rd,jde->jre/dot_general | solution.py:51
  32.9 4.3 %collective-permute-done.1 = bf16[64,3072]{1,0:T(8,128)(2,1)S(1)} collective-permute-done((bf16[64,3072]{1,0:T(8,128)(2,1)S(1)}, bf16[64,3072]{1,0:T(8,128)(2,1)S(1)}, u32[]{:S(2)}, u32[]{:S(2)}) %collective-permute-start.1) | collective-permute-done | bytes 393248 | tf_op jit(solution)/shard_map/ppermute | solution.py:23
  37.3 7.6 %convolution_bitcast_fusion.1 = f32[1,3,64,768]{3,2,1,0:T(8,128)S(1)} fusion(bf16[3,3072,768]{2,1,0:T(8,128)(2,1)} %param.14, bf16[64,3072]{1,0:T(8,128)(2,1)S(1)} %collective-permute-done.1), kind=kOutput, calls=%fused_computation.18 | convolution fusion | flops 905969664 | bytes 15138816 | tf_op jit(solution)/shard_map/rd,jde->jre/dot_general | solution.py:51
  44.8 3.7 %collective-permute-done.2 = bf16[64,3072]{1,0:T(8,128)(2,1)S(1)} collective-permute-done((bf16[64,3072]{1,0:T(8,128)(2,1)S(1)}, bf16[64,3072]{1,0:T(8,128)(2,1)S(1)}, u32[]{:S(2)}, u32[]{:S(2)}) %collective-permute-start.2) | collective-permute-done | bytes 393248 | tf_op jit(solution)/shard_map/ppermute | solution.py:23
  48.5 2.5 %convolution_bitcast_fusion = f32[1,3,64,768]{3,2,1,0:T(8,128)S(1)} fusion(bf16[3,3072,768]{2,1,0:T(8,128)(2,1)S(1)} %bitcast.108, bf16[64,3072]{1,0:T(8,128)(2,1)S(1)} %collective-permute-done.2), kind=kOutput, calls=%fused_computation.17 | convolution fusion | flops 905969664 | bytes 15138816 | tf_op jit(solution)/shard_map/rd,jde->jre/dot_general | solution.py:51
  51.3 2.2 %gather_fusion = f32[4,3,64,768]{3,2,1,0:T(8,128)} fusion(f32[4,3,64,768]{3,2,1,0:T(8,128)S(1)} %pad_maximum_fusion, s32[1024]{0:T(1024)S(1)} %pad_clamp_fusion), kind=kCustom, calls=%fused_computation | custom fusion | bytes 4718608 | tf_op jit(solution)/shard_map/gather | solution.py:26
  53.4 1.2 slice.35
  54.6 0.9 copy.38
  55.7 1.7 slice_multiply_fusion
  57.3 1.2 copy.35
  59.1 2.1 %fusion.17 = bf16[1,256,768]{1,2,0:T(8,128)(2,1)} fusion(f32[1,256,768]{1,2,0:T(8,128)} %copy.35, f32[768]{0:T(1024)S(1)} %broadcast_bitcast_fusion.1, f32[256,6]{0,1:T(8,128)S(1)} %add_rsqrt_fusion.1), kind=kLoop, calls=%fused_computation.38 | loop fusion | flops 589824 | bytes 1188864 | tf_op jit(solution)/shard_map/slice | solution.py:58
  62.7 23.5 %all-gather.5.cloned.1.call-done = bf16[2048,768]{0,1:T(8,128)(2,1)} async-done(((bf16[256,768]{0,1:T(8,128)(2,1)}), bf16[2048,768]{0,1:T(8,128)(2,1)}) %all-gather.5.cloned.1.call-update) | async-done | bytes 3145744 | tf_op jit(solution)/shard_map/all_gather | solution.py:67
  86.3 34.6 %all-gather.9.cloned.1.call-done = bf16[1,2048,768]{1,2,0:T(8,128)(2,1)} async-done(((bf16[1,256,768]{1,2,0:T(8,128)(2,1)}), bf16[1,2048,768]{1,2,0:T(8,128)(2,1)}) %all-gather.9.cloned.1.call-update) | async-done | bytes 3145744 | tf_op jit(solution)/shard_map/all_gather | solution.py:66
  120.9 20.8 %while.18 = (s32[]{:T(128)}, f32[6,256]{1,0:T(8,128)S(1)}, f32[6,256]{1,0:T(8,128)S(1)}, f32[6,256,128]{2,1,0:T(8,128)S(1)}, bf16[2048,768]{0,1:T(8,128)(2,1)}, ...) while((s32[]{:T(128)}, f32[6,256]{1,0:T(8,128)S(1)}, ...), condition=%wide.region_7.8_spmd.clone, body=%wide.region_4.7_spmd.clone.sunk | while | flops 203890176 | bytes 9142451 | solution.py:91
  120.9 1.2 constant_dynamic-slice_fusion.3
  122.1 0.4 bitcast_reduce_fusion.2
  122.8 0.7 convolution_add_fusion.2
  123.5 1.2 constant_dynamic-slice_fusion.3
  125.4 0.7 convolution_add_fusion.2
  126.1 1.2 constant_dynamic-slice_fusion.3
  127.3 0.4 bitcast_reduce_fusion.2
  128.0 0.7 convolution_add_fusion.2
  128.7 1.2 constant_dynamic-slice_fusion.3
  129.9 0.4 bitcast_reduce_fusion.2
  130.6 0.7 convolution_add_fusion.2
  131.3 1.2 constant_dynamic-slice_fusion.3
  132.5 0.4 bitcast_reduce_fusion.2
  133.2 0.7 convolution_add_fusion.2
  133.9 1.2 constant_dynamic-slice_fusion.3
  135.1 0.4 bitcast_reduce_fusion.2
  135.8 0.7 convolution_add_fusion.2
  136.5 1.2 constant_dynamic-slice_fusion.3
  137.7 0.4 bitcast_reduce_fusion.2
  138.4 0.7 convolution_add_fusion.2
  139.1 1.2 constant_dynamic-slice_fusion.3
  141.0 0.7 convolution_add_fusion.2
  141.9 0.8 divide_convert_fusion
  142.8 37.2 %all-gather.7.cloned.1.call-done = bf16[256,3072]{0,1:T(8,128)(2,1)} async-done(((bf16[256,768]{0,1:T(8,128)(2,1)}), bf16[256,3072]{0,1:T(8,128)(2,1)}) %all-gather.7.cloned.1.call-update) | async-done | bytes 1572880 | tf_op jit(solution)/shard_map/all_gather | solution.py:95
  180.0 4.2 %convolution_convert_fusion = bf16[256,768]{1,0:T(8,128)(2,1)S(1)} fusion(bf16[256,3072]{0,1:T(8,128)(2,1)} %all-gather.7.cloned.1.call-done, bf16[3072,768]{1,0:T(8,128)(2,1)} %param.17), kind=kOutput, calls=%fused_computation.16 | convolution fusion | flops 1208156160 | bytes 6684672 | tf_op jit(solution)/shard_map/dot_general | solution.py:94
  184.2 14.1 %all_to_all.13 = bf16[4,64,768]{2,1,0:T(8,128)(2,1)S(1)} all-to-all(bf16[4,64,768]{2,1,0:T(8,128)(2,1)S(1)} %bitcast.120), channel_id=1, replica_groups=mesh['blk'=8,'ulysses'=4] {'ulysses'}, dimensions={0} | all-to-all | bytes 786432 | tf_op jit(solution)/shard_map/all_to_all | solution.py:99
  198.4 0.8 fusion.12
  (83 shorter events, 5.6 us)
Async XLA Ops:
  6.5 49.1 %copy-start = (f32[128]{0:T(128)S(1)}, f32[128]{0:T(128)}, u32[]{:S(2)}) copy-start(f32[128]{0:T(128)} %param.16) | copy-start | bytes 1540
  6.5 79.7 %all-gather.5.cloned.1.call-start = ((), (), s32[]{:S(2)}) async-start(), calls=%async_computation.1 | async-start | bytes 3538944 | tf_op jit(solution)/shard_map/all_gather | solution.py:67
  10.9 14.2 %collective-permute-start = (bf16[64,3072]{1,0:T(8,128)(2,1)S(1)}, bf16[64,3072]{1,0:T(8,128)(2,1)S(1)}, u32[]{:S(2)}, u32[]{:S(2)}) collective-permute-start(bf16[64,3072]{1,0:T(8,128)(2,1)S(1)} %fusion.11), channel_id=1, source_target_pairs={{0,1},{1,2},{2,3},{3,0},{4,5},{5,6},{6,7},{7,4},{8,9},{9,10},{10,1... | collective-permute-start | bytes 1179656 | tf_op jit(solution)/shard_map/ppermute | solution.py:23
  25.2 12.1 %collective-permute-start.1 = (bf16[64,3072]{1,0:T(8,128)(2,1)S(1)}, bf16[64,3072]{1,0:T(8,128)(2,1)S(1)}, u32[]{:S(2)}, u32[]{:S(2)}) collective-permute-start(bf16[64,3072]{1,0:T(8,128)(2,1)S(1)} %collective-permute-done), channel_id=1, source_target_pairs={{0,1},{1,2},{2,3},{3,0},{4,5},{5,6},{6,7},{7,4},{8,9},{9,10},{10,1... | collective-permute-start | bytes 1179656 | tf_op jit(solution)/shard_map/ppermute | solution.py:23
  25.2 23.3 %slice-start = ((s8[14155776]{0:T(1024)(128)(4,1)}), s8[4194304]{0:T(1024)(128)(4,1)S(1)}, s32[]{:S(2)}) async-start(s8[14155776]{0:T(1024)(128)(4,1)} %bitcast.107), calls=%async_computation.4 | async-start | bytes 8388608
  25.2 23.3 %slice-start.1 = ((s8[14155776]{0:T(1024)(128)(4,1)}), s8[4194304]{0:T(1024)(128)(4,1)S(1)}, s32[]{:S(2)}) async-start(s8[14155776]{0:T(1024)(128)(4,1)} %bitcast.107), calls=%async_computation.5 | async-start | bytes 8388608
  32.9 15.6 %slice-start.2 = ((s8[14155776]{0:T(1024)(128)(4,1)}), s8[4194304]{0:T(1024)(128)(4,1)S(1)}, s32[]{:S(2)}) async-start(s8[14155776]{0:T(1024)(128)(4,1)} %bitcast.107), calls=%async_computation.6 | async-start | bytes 8388608
  32.9 15.6 %slice-start.3 = ((s8[14155776]{0:T(1024)(128)(4,1)}), s8[1572864]{0:T(1024)(128)(4,1)S(1)}, s32[]{:S(2)}) async-start(s8[14155776]{0:T(1024)(128)(4,1)} %bitcast.107), calls=%async_computation.7 | async-start | bytes 3145728
  37.3 11.2 %collective-permute-start.2 = (bf16[64,3072]{1,0:T(8,128)(2,1)S(1)}, bf16[64,3072]{1,0:T(8,128)(2,1)S(1)}, u32[]{:S(2)}, u32[]{:S(2)}) collective-permute-start(bf16[64,3072]{1,0:T(8,128)(2,1)S(1)} %collective-permute-done.1), channel_id=1, source_target_pairs={{0,1},{1,2},{2,3},{3,0},{4,5},{5,6},{6,7},{7,4},{8,9},{9,10},{10,1... | collective-permute-start | bytes 1179656 | tf_op jit(solution)/shard_map/ppermute | solution.py:23
  55.6 65.3 %all-gather.9.cloned.1.call-start = ((), (), s32[]{:S(2)}) async-start(), calls=%async_computation.3 | async-start | bytes 3538944 | tf_op jit(solution)/shard_map/all_gather | solution.py:66
  58.5 2.9 %copy-start.3 = (f32[128]{0:T(128)S(1)}, f32[128]{0:T(128)}, u32[]{:S(2)}) copy-start(f32[128]{0:T(128)} %param.15) | copy-start | bytes 1540
  61.2 118.8 %all-gather.7.cloned.1.call-start = ((), (), s32[]{:S(2)}) async-start(), calls=%async_computation.2 | async-start | bytes 1966080 | tf_op jit(solution)/shard_map/all_gather | solution.py:95
  184.2 14.2 %copy-start.1 = (bf16[64,3072]{1,0:T(8,128)(2,1)S(1)}, bf16[64,3072]{1,0:T(8,128)(2,1)}, u32[]{:S(2)}) copy-start(bf16[64,3072]{1,0:T(8,128)(2,1)} %param.10) | copy-start | bytes 1179652
  184.2 14.2 %copy-start.2 = (f32[3072]{0:T(1024)S(1)}, f32[3072]{0:T(1024)}, u32[]{:S(2)}) copy-start(f32[3072]{0:T(1024)} %param.13) | copy-start | bytes 36868
Sparse Core Ops, SparseCore 0:
  55.7 30.5 all-gather.4
  88.1 32.7 all-gather.8
  142.9 37.0 all-gather.6
